TPU v7x, 32 devices: a whole 2x2x4 slice. The times are simulated.
32 devices in a mesh: rep: 2 (over y), dev: 4 (over z), col: 4 (over x, core).
Axes of the slice: x: 2, y: 2, z: 4, core: 2. Of those that a mesh axis runs over, the one named last changes fastest.
Arguments:
- queries: bfloat16 [256, 8192], P(('rep', 'dev'), 'col'), parts along dimension 0
- kv_pages: bfloat16 [768, 8, 2, 128, 128], P(('rep', 'dev'), 'col'), parts along dimension 0
- page_table: int32 [256, 3], P(('rep', 'dev')), parts along dimension 0, may hold values from 0 to 95, as said below
- seq_lengths: int32 [256], P(('rep', 'dev')), parts along dimension 0, may hold values from 2 to 384, as said below
- ffn_seat: int32 [256], P('rep'), parts along dimension 0, may hold values from 0 to 127, each once
- resid: bfloat16 [256, 8192], P(('rep', 'col'), 'dev'), parts along dimension 0, may hold values from -6 to 6
- w_out: bfloat16 [8192, 8192], P('col', 'dev'), may hold values from -0.0625 to 0.0625
- norm_gain: float32 [8192], P('dev'), may hold values from 0.25 to 1.75
- w_gate: bfloat16 [8192, 14336], P('dev', 'col'), may hold values from -0.0625 to 0.0625
- w_up: bfloat16 [8192, 14336], P('dev', 'col'), may hold values from -0.0625 to 0.0625
- w_down: bfloat16 [14336, 8192], P('col', 'dev'), may hold values from -0.046875 to 0.046875
Outputs:
- layer_out: bfloat16 [256, 8192], P(('rep', 'col'), 'dev'), parts along dimension 0
There are 2 independent parts, one for each index of `rep`. A program takes and returns all parts, laid end to end along the dimension named above; an argument that names none is the same for every part. Nothing has to cross between parts.
Inputs may be any that keep to these rules, and one draw needn't show every extreme that they name: `page_table`: the 32 rows of one dev index hold each block 0 to 95 of that index's pool exactly once. `seq_lengths`: the first sequence has 384 cached tokens.
All inputs are finite; a program needn't handle non-finite values.
Results may differ from a plain program's by a relative error of at most 0.017.
Values may be sent and summed in bfloat16 or wider, within the bound.
A program may use at most 128 MiB of HBM per device.

v0:
```python
import jax
import jax.numpy as jnp
from jax import lax
from jax.sharding import PartitionSpec as P


def on_device(
    queries,
    kv_pages,
    page_table,
    seq_lengths,
    ffn_seat,
    resid,
    w_out,
    norm_gain,
    w_gate,
    w_up,
    w_down,
):
    seq_count = queries.shape[0]
    kv_local = kv_pages.shape[1]
    head_dim = kv_pages.shape[4]
    group_size = queries.shape[1] // (kv_local * head_dim)
    kv_blocks = kv_pages[page_table]
    key_span = kv_blocks.shape[1] * kv_blocks.shape[4]
    key_rows = (
        kv_blocks[:, :, :, 0]
        .transpose(0, 2, 1, 3, 4)
        .reshape(seq_count, kv_local, key_span, head_dim)
    )
    value_rows = (
        kv_blocks[:, :, :, 1]
        .transpose(0, 2, 1, 3, 4)
        .reshape(seq_count, kv_local, key_span, head_dim)
    )
    query_heads = queries.reshape(seq_count, kv_local, group_size, head_dim)
    scores = jnp.einsum(
        "skgd,sktd->skgt", query_heads, key_rows, preferred_element_type=jnp.float32
    ) * head_dim ** (-0.5)
    live_mask = jnp.arange(key_span)[None, :] < seq_lengths[:, None]
    scores = jnp.where(live_mask[:, None, None, :], scores, -1e30)
    top = jnp.max(scores, axis=-1, keepdims=True)
    expo = jnp.exp(scores - top)
    weights = (expo / jnp.sum(expo, axis=-1, keepdims=True)).astype(jnp.bfloat16)
    attended = jnp.einsum(
        "skgt,sktd->skgd", weights, value_rows, preferred_element_type=jnp.float32
    )
    attended = attended.astype(jnp.bfloat16).reshape(seq_count, -1)
    projected = jnp.dot(
        lax.all_gather(attended, "dev", axis=0, tiled=True),
        w_out,
        preferred_element_type=jnp.float32,
    )
    placed = jnp.zeros_like(projected).at[ffn_seat].set(projected)
    update = lax.psum_scatter(
        placed.astype(jnp.bfloat16), "col", scatter_dimension=0, tiled=True
    ).astype(jnp.float32)
    stream = resid.astype(jnp.float32) + update
    sq_total = lax.psum(jnp.sum(stream * stream, axis=1), "dev")
    full_width = stream.shape[1] * lax.axis_size("dev")
    normed = (
        stream * lax.rsqrt(sq_total / full_width + 1e-05)[:, None] * norm_gain[None, :]
    ).astype(jnp.bfloat16)
    block_rows = lax.all_gather(normed, "col", axis=0, tiled=True)
    gate_part = jnp.dot(block_rows, w_gate, preferred_element_type=jnp.float32)
    up_part = jnp.dot(block_rows, w_up, preferred_element_type=jnp.float32)
    gate_up = jnp.concatenate([gate_part, up_part], axis=1)
    half_width = w_gate.shape[1]
    shared_sums = lax.psum_scatter(
        gate_up.astype(jnp.bfloat16), "dev", scatter_dimension=0, tiled=True
    ).astype(jnp.float32)
    hidden_share = (jax.nn.silu(shared_sums[:, :half_width]) * shared_sums[:, half_width:]).astype(
        jnp.bfloat16
    )
    hidden = lax.all_gather(hidden_share, "dev", axis=0, tiled=True)
    ffn_out = lax.psum_scatter(
        jnp.dot(hidden, w_down, preferred_element_type=jnp.float32).astype(jnp.bfloat16),
        "col",
        scatter_dimension=0,
        tiled=True,
    ).astype(jnp.float32)
    return (stream + ffn_out).astype(jnp.bfloat16)


def solution(mesh):
    in_specs = (
        P(("rep", "dev"), "col"),
        P(("rep", "dev"), "col", None, None, None),
        P(("rep", "dev"), None),
        P(("rep", "dev")),
        P("rep"),
        P(("rep", "col"), "dev"),
        P("col", "dev"),
        P("dev"),
        P("dev", "col"),
        P("dev", "col"),
        P("col", "dev"),
    )
    out_specs = P(("rep", "col"), "dev")
    return jax.shard_map(
        on_device, mesh=mesh, in_specs=in_specs, out_specs=out_specs, check_vma=False
    )
```

profile of v0, /device:TPU:0, one launch (start us, length us, event | category | flops | bytes accessed | tf_op | source)
XLA Modules:
  0.0 218.6 jit_solution(14444316653443344116)
XLA Ops:
  6.5 0.0 reduce-scatter.4.cloned.1.call-start
  6.5 0.7 compare_select_fusion
  7.2 0.1 copy.15
  7.3 0.1 reshape.39
  7.4 11.5 %gather_fusion = bf16[96,2,2,128,128]{4,3,2,1,0:T(8,128)(2,1)} fusion(bf16[96,2,2,128,128]{4,3,2,1,0:T(8,128)(2,1)} %param.12, s32[1024]{0:T(1024)S(1)} %pad_clamp_fusion), kind=kCustom, calls=%fused_computation | custom fusion | bytes 25166208 | tf_op jit(solution)/shard_map/gather | solution.py:24
  18.9 5.3 %fusion.9 = (bf16[32,3,2,1,128,128]{5,4,3,2,1,0:T(8,128)(2,1)S(1)}, bf16[32,3,2,1,128,128]{5,4,3,2,1,0:T(8,128)(2,1)S(1)}) fusion(bf16[32,3,2,2,128,128]{5,4,3,2,1,0:T(8,128)(2,1)} %bitcast.34), kind=kLoop, calls=%fused_computation.29 | loop fusion | bytes 25165824 | tf_op jit(solution)/shard_map/slice | solution.py:27
  24.2 0.0 copy-start.3
  24.2 0.0 copy-start.5
  24.3 2.6 %copy.18 = bf16[32,3,2,1,128,128]{5,4,1,2,0,3:T(8,128)(2,1)S(1)} copy(bf16[32,3,2,1,128,128]{5,4,3,2,1,0:T(8,128)(2,1)S(1)} %get-tuple-element.5) | data formatting | bytes 12582912
  26.9 0.0 copy-done.3
  26.9 0.0 copy-done.5
  26.9 0.1 iota_compare_fusion
  27.0 2.3 %fusion.4 = f32[32,2,8,384]{3,2,1,0:T(8,128)S(1)} fusion(bf16[32,2,384,128]{3,2,1,0:T(8,128)(2,1)S(1)} %bitcast.35, bf16[32,2,8,128]{3,2,1,0:T(8,128)(2,1)S(1)} %bitcast.37, pred[32,384]{1,0:T(8,128)(4,1)S(1)} %iota_compare_fusion), kind=kOutput, calls=%fused_computation.11 | convolution fusion | flops 50724864 | bytes 7221248 | tf_op jit(solution)/shard_map/skgd,sktd->skgt/dot_general | solution.py:37
  29.3 0.0 copy-start
  29.3 0.3 fusion.10
  29.6 0.0 copy-start.6
  29.6 4.0 %copy.19 = bf16[32,3,2,1,128,128]{5,4,1,2,0,3:T(8,128)(2,1)} copy(bf16[32,3,2,1,128,128]{5,4,3,2,1,0:T(8,128)(2,1)S(1)} %get-tuple-element.6) | data formatting | bytes 12582912
  33.6 0.0 copy-done
  33.7 4.5 %convolution_convert_fusion.3 = bf16[32,2,8,128]{3,2,1,0:T(8,128)(2,1)S(1)} fusion(bf16[32,2,384,128]{3,2,1,0:T(8,128)(2,1)} %bitcast.36, f32[32,2,8]{2,1,0:T(2,128)S(1)} %fusion.10, f32[32,2,8,384]{3,2,1,0:T(8,128)} %copy-done), kind=kOutput, calls=%fused_computation.12 | convolution fusion | flops 50987904 | bytes 7211008 | tf_op jit(solution)/shard_map/skgt,sktd->skgd/dot_general | solution.py:45
  38.2 0.1 copy.23
  38.2 17.4 %all_gather.9 = bf16[128,2048]{1,0:T(8,128)(2,1)S(1)} all-gather(bf16[32,2048]{1,0:T(8,128)(2,1)S(1)} %bitcast.38), channel_id=1, replica_groups=mesh['rep'=2,'dev'=4,'col'=4] {'dev'}, dimensions={0}, use_global_device_ids=true | all-gather | bytes 655360 | tf_op jit(solution)/shard_map/all_gather | solution.py:50
  55.6 0.0 copy-done.6
  55.6 4.7 %fusion.11 = f32[128,2048]{1,0:T(8,128)S(1)} fusion(bf16[128,2048]{1,0:T(8,128)(2,1)S(1)} %all_gather.9, bf16[2048,2048]{1,0:T(8,128)(2,1)} %param.17), kind=kOutput, calls=%fused_computation.31 | convolution fusion | flops 1073741824 | bytes 9961472 | tf_op jit(solution)/shard_map/dot_general | solution.py:49
  60.3 1.5 scatter_custom_fusion
  61.8 0.9 convert_element_type.37
  62.7 0.0 reduce-scatter.4.cloned.1.call-update
  62.7 0.0 reduce-scatter.6.cloned.1.call-start
  62.8 23.5 %reduce-scatter.4.cloned.1.call-done = bf16[32,2048]{1,0:T(8,128)(2,1)} async-done(((bf16[128,2048]{1,0:T(8,128)(2,1)}), bf16[32,2048]{1,0:T(8,128)(2,1)}) %reduce-scatter.4.cloned.1.call-update) | async-done | bytes 131088 | tf_op jit(solution)/shard_map/reduce_scatter | solution.py:55
  86.3 0.0 copy-done.1
  86.3 1.1 multiply_reduce_fusion
  87.3 11.7 %psum.7 = f32[32]{0:T(128)S(1)} all-reduce(f32[32]{0:T(128)S(1)} %multiply_reduce_fusion), channel_id=1, replica_groups=mesh['rep'=2,'dev'=4,'col'=4] {'dev'}, use_global_device_ids=true, to_apply=%region_5.6 | all-reduce | flops 32 | bytes 256 | tf_op jit(solution)/shard_map/psum | solution.py:59
  99.0 0.0 copy-done.4
  99.0 1.0 multiply_convert_fusion
  100.0 6.7 %all_gather.10 = bf16[128,2048]{1,0:T(8,128)(2,1)S(1)} all-gather(bf16[32,2048]{1,0:T(8,128)(2,1)S(1)} %multiply_convert_fusion), channel_id=1, replica_groups=mesh['rep'=2,'dev'=4,'col'=4] {'col'}, dimensions={0}, use_global_device_ids=true | all-gather | bytes 655360 | tf_op jit(solution)/shard_map/all_gather | solution.py:64
  106.7 7.3 %convolution_convert_fusion = bf16[128,3584]{1,0:T(8,128)(2,1)S(1)} fusion(bf16[128,2048]{1,0:T(8,128)(2,1)S(1)} %all_gather.10, bf16[2048,3584]{1,0:T(8,128)(2,1)} %param.20), kind=kOutput, calls=%fused_computation.3 | convolution fusion | flops 1879506944 | bytes 16121856 | tf_op jit(solution)/shard_map/dot_general | solution.py:66
  114.0 7.3 %convolution_convert_fusion.1 = bf16[128,3584]{1,0:T(8,128)(2,1)S(1)} fusion(bf16[128,2048]{1,0:T(8,128)(2,1)S(1)} %all_gather.10, bf16[2048,3584]{1,0:T(8,128)(2,1)} %param.19), kind=kOutput, calls=%fused_computation.4 | convolution fusion | flops 1879506944 | bytes 16121856 | tf_op jit(solution)/shard_map/dot_general | solution.py:65
  121.3 1.4 pad_maximum_fusion
  122.7 0.0 reduce-scatter.6.cloned.1.call-update
  122.7 0.0 reduce-scatter.8.cloned.1.call-start
  122.8 37.5 %reduce-scatter.6.cloned.1.call-done = bf16[32,7168]{1,0:T(8,128)(2,1)} async-done(((bf16[128,7168]{1,0:T(8,128)(2,1)}), bf16[32,7168]{1,0:T(8,128)(2,1)}) %reduce-scatter.6.cloned.1.call-update) | async-done | bytes 458768 | tf_op jit(solution)/shard_map/reduce_scatter | solution.py:69
  160.3 1.1 convert_element_type.40
  161.4 0.1 fusion.7
  161.5 19.1 %all_gather.11 = bf16[128,3584]{1,0:T(8,128)(2,1)S(1)} all-gather(bf16[32,3584]{1,0:T(8,128)(2,1)S(1)} %fusion.7), channel_id=1, replica_groups=mesh['rep'=2,'dev'=4,'col'=4] {'dev'}, dimensions={0}, use_global_device_ids=true | all-gather | bytes 1146880 | tf_op jit(solution)/shard_map/all_gather | solution.py:75
  180.6 8.3 %convolution_convert_fusion.2 = bf16[128,2048]{1,0:T(8,128)(2,1)} fusion(bf16[128,3584]{1,0:T(8,128)(2,1)S(1)} %all_gather.11, bf16[3584,2048]{1,0:T(8,128)(2,1)} %param.21), kind=kOutput, calls=%fused_computation.5 | convolution fusion | flops 1879310336 | bytes 16121856 | tf_op jit(solution)/shard_map/dot_general | solution.py:77
  188.9 0.0 reduce-scatter.8.cloned.1.call-update
  189.0 21.5 %reduce-scatter.8.cloned.1.call-done = bf16[32,2048]{1,0:T(8,128)(2,1)} async-done(((bf16[128,2048]{1,0:T(8,128)(2,1)}), bf16[32,2048]{1,0:T(8,128)(2,1)}) %reduce-scatter.8.cloned.1.call-update) | async-done | bytes 131088 | tf_op jit(solution)/shard_map/reduce_scatter | solution.py:76
  210.4 0.0 copy-done.2
  210.4 1.6 add_convert_fusion
  (7 shorter events, 0.0 us)
Async XLA Ops:
  6.5 79.7 %reduce-scatter.4.cloned.1.call-start = ((), (), s32[]{:S(2)}) async-start(), calls=%async_computation.3 | async-start | bytes 655360 | tf_op jit(solution)/shard_map/reduce_scatter | solution.py:55
  24.2 2.7 %copy-start.3 = (bf16[32,2048]{1,0:T(8,128)(2,1)S(1)}, bf16[32,2048]{1,0:T(8,128)(2,1)}, u32[]{:S(2)}) copy-start(bf16[32,2048]{1,0:T(8,128)(2,1)} %param.11) | copy-start | bytes 393220
  24.2 2.7 %copy-start.5 = (s32[32]{0:T(128)S(1)}, s32[32]{0:T(128)}, u32[]{:S(2)}) copy-start(s32[32]{0:T(128)} %param.14) | copy-start | bytes 388
  29.3 4.4 %copy-start = (f32[32,2,8,384]{3,2,1,0:T(8,128)}, f32[32,2,8,384]{3,2,1,0:T(8,128)S(1)}, u32[]{:S(2)}) copy-start(f32[32,2,8,384]{3,2,1,0:T(8,128)S(1)} %fusion.4) | copy-start | bytes 2359300
  29.6 26.0 %copy-start.6 = (s32[128]{0:T(128)S(1)}, s32[128]{0:T(128)}, u32[]{:S(2)}) copy-start(s32[128]{0:T(128)} %param.15) | copy-start | bytes 1540
  55.6 30.7 %copy-start.1 = (bf16[32,2048]{1,0:T(8,128)(2,1)S(1)}, bf16[32,2048]{1,0:T(8,128)(2,1)}, u32[]{:S(2)}) copy-start(bf16[32,2048]{1,0:T(8,128)(2,1)} %param.16) | copy-start | bytes 393220
  55.6 43.4 %copy-start.4 = (f32[2048]{0:T(1024)S(1)}, f32[2048]{0:T(1024)}, u32[]{:S(2)}) copy-start(f32[2048]{0:T(1024)} %param.18) | copy-start | bytes 24580
  62.7 97.6 %reduce-scatter.6.cloned.1.call-start = ((), (), s32[]{:S(2)}) async-start(), calls=%async_computation.4 | async-start | bytes 2293760 | tf_op jit(solution)/shard_map/reduce_scatter | solution.py:69
  122.7 87.7 %reduce-scatter.8.cloned.1.call-start = ((), (), s32[]{:S(2)}) async-start(), calls=%async_computation.5 | async-start | bytes 655360 | tf_op jit(solution)/shard_map/reduce_scatter | solution.py:76
  180.6 29.9 %copy-start.2 = (bf16[32,2048]{1,0:T(8,128)(2,1)S(1)}, bf16[32,2048]{1,0:T(8,128)(2,1)}, u32[]{:S(2)}) copy-start(bf16[32,2048]{1,0:T(8,128)(2,1)} %reduce-scatter.4.cloned.1.call-done) | copy-start | bytes 393220
Sparse Core Ops, SparseCore 0:
  62.8 23.4 reduce-scatter.3
  122.8 37.3 reduce-scatter.5
  189.1 21.3 reduce-scatter.7
where the time goes:
time: 219 us
  waiting for transfers between devices  82.6 us (38%)
  blocking collectives  54.8 us (25%)
  matrix products  34.4 us (16%)
  local copies, waits for them, and re-layouts  25.2 us (12%)
  between operations  13.3 us (6%)
  other arithmetic  8.25 us (4%)
    reduce_scatter x1, waiting for transfers between devices, on_device(): lax.psum_scatter(gate_up.astype(jnp.bfloat16), 'dev', scatter_dimension=0...  37.5 us
    reduce_scatter x1, waiting for transfers between devices, on_device(): lax.psum_scatter(placed.astype(jnp.bfloat16), 'col', scatter_dimension=0,...  23.5 us
    reduce_scatter x1, waiting for transfers between devices, on_device(): lax.psum_scatter(jnp.dot(hidden, w_down, preferred_element_type=jnp.float...  21.5 us
    all_gather x1, blocking collectives, on_device(): hidden = lax.all_gather(hidden_share, 'dev', axis=0, tiled=True)  19.1 us
    all_gather x1, blocking collectives, on_device(): lax.all_gather(attended, 'dev', axis=0, tiled=True)  17.4 us
    psum x1, blocking collectives, on_device(): sq_total = lax.psum(jnp.sum(stream * stream, axis=1), 'dev')  11.7 us
    gather x1, local copies, waits for them, and re-layouts, on_device(): kv_blocks = kv_pages[page_table]  11.5 us
    dot_general x1, matrix products, on_device(): jnp.dot(hidden, w_down, preferred_element_type=jnp.float32)  8.35 us
  transfers between devices with their start and end apart: 3, of which 3 were waited for; matrix products, arithmetic and copies ran while one was open for 0% of the time, Pallas kernels for 0%

commit v1 on v0

v1 whole, which is shorter than its diff:
```python
import functools

import jax
import jax.numpy as jnp
from jax import lax
from jax.experimental import pallas as pl
from jax.experimental.pallas import tpu as pltpu
from jax.sharding import PartitionSpec as P

MESH = pl.DeviceIdType.MESH
F32 = jnp.float32
BF16 = jnp.bfloat16


def divisor(size, choices):
    for choice in choices:
        if size % choice == 0:
            return choice
    return size


def attend_kernel(seqs, pages, kv_local, table_ref, len_ref, q_ref, *refs):
    blocks, out_ref = refs[:-1], refs[-1]
    step = pl.program_id(0)
    page, head_dim = blocks[0].shape[3], blocks[0].shape[4]
    span = pages * page
    scale = head_dim ** (-0.5)
    for s in range(seqs):
        length = len_ref[step * seqs + s]
        for h in range(kv_local):
            query = q_ref[s, h]
            scores = jnp.concatenate(
                [
                    lax.dot_general(
                        query,
                        blocks[s * pages + j][0, h, 0],
                        (((1,), (1,)), ((), ())),
                        preferred_element_type=F32,
                    )
                    for j in range(pages)
                ],
                axis=1,
            ) * scale
            live = lax.broadcasted_iota(jnp.int32, scores.shape, 1) < length
            scores = jnp.where(live, scores, -1e30)
            top = jnp.max(scores, axis=1, keepdims=True)
            expo = jnp.exp(scores - top)
            weights = (expo / jnp.sum(expo, axis=1, keepdims=True)).astype(BF16)
            total = None
            for j in range(pages):
                part = jnp.dot(
                    weights[:, j * page : (j + 1) * page],
                    blocks[s * pages + j][0, h, 1],
                    preferred_element_type=F32,
                )
                total = part if total is None else total + part
            out_ref[s, h] = total.astype(BF16)


def attend(queries, kv_pages, page_table, seq_lengths):
    count = queries.shape[0]
    _, kv_local, _, page, head_dim = kv_pages.shape
    pages = page_table.shape[1]
    group = queries.shape[1] // (kv_local * head_dim)
    seqs = divisor(count, (4, 2, 1))

    def block_map(s, j, i, table, lens):
        return (table[(i * seqs + s) * pages + j], 0, 0, 0, 0)

    kv_specs = [
        pl.BlockSpec((1, kv_local, 2, page, head_dim), functools.partial(block_map, s, j))
        for s in range(seqs)
        for j in range(pages)
    ]
    q_spec = pl.BlockSpec((seqs, kv_local, group, head_dim), lambda i, table, lens: (i, 0, 0, 0))
    out = pl.pallas_call(
        functools.partial(attend_kernel, seqs, pages, kv_local),
        grid_spec=pltpu.PrefetchScalarGridSpec(
            num_scalar_prefetch=2,
            grid=(count // seqs,),
            in_specs=[q_spec] + kv_specs,
            out_specs=q_spec,
        ),
        out_shape=jax.ShapeDtypeStruct((count, kv_local, group, head_dim), BF16),
        compiler_params=pltpu.CompilerParams(dimension_semantics=("arbitrary",)),
    )(
        page_table.reshape(-1),
        seq_lengths,
        queries.reshape(count, kv_local, group, head_dim),
        *([kv_pages] * len(kv_specs)),
    )
    return out.reshape(count, -1)


def layer_kernel(
    nd,
    nc,
    dims,
    att_ref,
    seat_ref,
    resid_ref,
    gain_ref,
    wo_hbm,
    wg_hbm,
    wu_hbm,
    wd_hbm,
    out_ref,
    wo,
    wg,
    wu,
    wd,
    att_all,
    seated,
    proj,
    rs_in,
    x_all,
    ss_all,
    stream,
    own,
    in_r,
    in_l,
    ss_own,
    ss_r,
    ss_l,
    inv,
    hid,
    acc,
    down,
    down_in,
    w_sem,
    f_sem,
    att_s,
    att_r,
    rs_s,
    rs_r,
    x_s,
    x_r,
    ssc_s,
    ssc_r,
    sum_s,
    sum_r,
    ssd_s,
    ssd_r,
    hid_s,
    hid_r,
    dn_s,
    dn_r,
):
    T, B, R, HK, WC, NJ, AC, NA, CF, NC, half, full = dims
    me = lax.axis_index("dev")
    mc = lax.axis_index("col")
    E = nd - 1

    def peer_of(k):
        return lax.rem(mc + k, nc)

    def wo_copy(j):
        cols = pl.ds(pl.multiple_of(j * WC, WC), WC)
        return pltpu.make_async_copy(wo_hbm.at[:, cols], wo.at[j], w_sem.at[j])

    def ffn_copy(which, c):
        span = pl.ds(pl.multiple_of(c * CF, CF), CF)
        source = (wg_hbm.at[:, span], wu_hbm.at[:, span], wd_hbm.at[span, :])[which]
        return pltpu.make_async_copy(source, (wg, wu, wd)[which].at[c], f_sem.at[which, c])

    @pl.loop(0, NJ)
    def _(j):
        wo_copy(j).start()

    @pl.loop(0, NC)
    def _(c):
        ffn_copy(0, c).start()
        ffn_copy(1, c).start()

    @pl.loop(0, NC)
    def _(c):
        ffn_copy(2, c).start()

    barrier = pltpu.get_barrier_semaphore()

    @pl.when(me > 0)
    def _():
        pl.semaphore_signal(barrier, inc=1, device_id={"dev": me - 1}, device_id_type=MESH)

    @pl.when(me < E)
    def _():
        pl.semaphore_signal(barrier, inc=1, device_id={"dev": me + 1}, device_id_type=MESH)

    for k in range(1, nc):
        pl.semaphore_signal(barrier, inc=1, device_id={"col": peer_of(k)}, device_id_type=MESH)

    neighbours = jnp.where(me > 0, 1, 0) + jnp.where(me < E, 1, 0)
    pl.semaphore_wait(barrier, neighbours + (nc - 1))

    def att_rows(origin):
        return pl.ds(pl.multiple_of(origin * B, B), B)

    def att_copy(origin, a, way, from_input):
        cols = slice(a * AC, (a + 1) * AC)
        dst = att_all.at[att_rows(origin), cols]
        return pltpu.make_async_remote_copy(
            src_ref=att_ref.at[:, cols] if from_input else dst,
            dst_ref=dst,
            send_sem=att_s.at[way, origin, a],
            recv_sem=att_r.at[origin, a],
            device_id={"dev": me + (1 if way == 0 else -1)},
            device_id_type=MESH,
        )

    for a in range(NA):
        @pl.when(me < E)
        def _():
            att_copy(me, a, 0, True).start()

        @pl.when(me > 0)
        def _():
            att_copy(me, a, 1, True).start()

    att_all[att_rows(me), :] = att_ref[...]

    @pl.loop(1, nd)
    def _(k):
        for a in range(NA):
            @pl.when(me - k >= 0)
            def _():
                att_copy(me - k, a, 0, False).wait_recv()

                @pl.when(me < E)
                def _():
                    att_copy(me - k, a, 0, False).start()

            @pl.when(me + k <= E)
            def _():
                att_copy(me + k, a, 1, False).wait_recv()

                @pl.when(me > 0)
                def _():
                    att_copy(me + k, a, 1, False).start()

    pick = (lax.broadcasted_iota(jnp.int32, (T, T), 0) == seat_ref[...]).astype(F32).astype(BF16)
    seated[...] = jnp.dot(pick, att_all[...], preferred_element_type=F32).astype(BF16)

    def rs_copy(k, j, source, target, send, recv):
        cols = pl.ds(pl.multiple_of(j * WC, WC), WC)
        rows = pl.ds(pl.multiple_of(peer_of(k) * R, R), R)
        return pltpu.make_async_remote_copy(
            src_ref=source.at[rows, cols],
            dst_ref=target.at[k - 1, :, cols],
            send_sem=send.at[k - 1, j],
            recv_sem=recv.at[k - 1, j],
            device_id={"col": peer_of(k)},
            device_id_type=MESH,
        )

    @pl.loop(0, NJ)
    def _(j):
        wo_copy(j).wait()
        cols = pl.ds(pl.multiple_of(j * WC, WC), WC)
        proj[:, cols] = jnp.dot(seated[...], wo[j], preferred_element_type=F32).astype(BF16)
        for k in range(1, nc):
            rs_copy(k, j, proj, rs_in, rs_s, rs_r).start()

    my_rows = pl.ds(pl.multiple_of(mc * R, R), R)

    def x_copy(k, j):
        spot = x_all.at[my_rows, pl.ds(pl.multiple_of(j * WC, WC), WC)]
        return pltpu.make_async_remote_copy(
            src_ref=spot,
            dst_ref=spot,
            send_sem=x_s.at[k - 1, j],
            recv_sem=x_r.at[k - 1, j],
            device_id={"col": peer_of(k)},
            device_id_type=MESH,
        )

    def ssc_copy(k):
        spot = ss_all.at[my_rows, :]
        return pltpu.make_async_remote_copy(
            src_ref=spot,
            dst_ref=spot,
            send_sem=ssc_s.at[k - 1],
            recv_sem=ssc_r.at[k - 1],
            device_id={"col": peer_of(k)},
            device_id_type=MESH,
        )

    squares = jnp.zeros((R, 1), F32)
    for j in range(NJ):
        cols = slice(j * WC, (j + 1) * WC)
        value = resid_ref[:, cols].astype(F32) + proj[my_rows, cols].astype(F32)
        for k in range(1, nc):
            rs_copy(k, j, proj, rs_in, rs_s, rs_r).wait_recv()
            value = value + rs_in[k - 1, :, cols].astype(F32)
        stream[:, cols] = value
        squares = squares + jnp.sum(value * value, axis=1, keepdims=True)
        x_all[my_rows, cols] = (value * gain_ref[:, cols]).astype(BF16)
        for k in range(1, nc):
            x_copy(k, j).start()
    ss_all[my_rows, :] = jnp.broadcast_to(squares, (R, ss_all.shape[1]))
    for k in range(1, nc):
        ssc_copy(k).start()
    for k in range(1, nc):
        for j in range(NJ):
            x_copy(k, j).wait_recv()
        ssc_copy(k).wait_recv()
    ss_own[...] = ss_all[...]

    def neighbour(way):
        return {"dev": me + (1 if way == 0 else -1)}

    def sum_copy(way, c):
        return pltpu.make_async_remote_copy(
            src_ref=own.at[c, 1 - way],
            dst_ref=(in_r if way == 0 else in_l).at[c],
            send_sem=sum_s.at[way, c],
            recv_sem=sum_r.at[way, c],
            device_id=neighbour(way),
            device_id_type=MESH,
        )

    def ssd_copy(way):
        return pltpu.make_async_remote_copy(
            src_ref=ss_own.at[pl.ds((1 - way) * half, half), :],
            dst_ref=ss_r if way == 0 else ss_l,
            send_sem=ssd_s.at[way],
            recv_sem=ssd_r.at[way],
            device_id=neighbour(way),
            device_id_type=MESH,
        )

    def hid_copy(way, c):
        spot = hid.at[c, pl.ds(way * half, half), :]
        return pltpu.make_async_remote_copy(
            src_ref=spot,
            dst_ref=spot,
            send_sem=hid_s.at[way, c],
            recv_sem=hid_r.at[way, c],
            device_id=neighbour(way),
            device_id_type=MESH,
        )

    def sum_stage(way, c):
        first = 0 if way == 0 else E
        last = E - first
        part = 1 - way
        incoming = in_r if way == 0 else in_l
        ss_in = ss_r if way == 0 else ss_l
        ss_rows = pl.ds(part * half, half)

        @pl.when(c == 0)
        def _():
            @pl.when(me != first)
            def _():
                ssd_copy(way).wait_recv()
                ss_own[ss_rows, :] = ss_own[ss_rows, :] + ss_in[...]

            @pl.when(me != last)
            def _():
                ssd_copy(way).start()

            @pl.when(me == last)
            def _():
                inv[...] = lax.rsqrt(ss_own[ss_rows, :] / full + 1e-5)

        @pl.when(me != first)
        def _():
            sum_copy(way, c).wait_recv()

            @pl.when(me != last)
            def _():
                total = own[c, part].astype(F32) + incoming[c].astype(F32)
                own[c, part] = total.astype(BF16)

        @pl.when(me != last)
        def _():
            sum_copy(way, c).start()

        @pl.when(me == last)
        def _():
            total = own[c, part].astype(F32) + incoming[c].astype(F32)
            scale = inv[:, 0:1]
            gate = total[:, :CF] * scale
            up = total[:, CF:] * scale
            hid[c, part * half : (part + 1) * half, :] = (
                gate / (1.0 + jnp.exp(-gate)) * up
            ).astype(BF16)
            hid_copy(part, c).start()

    def hid_stage(way, c):
        first = 0 if way == 0 else E
        last = E - first

        @pl.when(me != first)
        def _():
            hid_copy(way, c).wait_recv()

            @pl.when(me != last)
            def _():
                hid_copy(way, c).start()

    def inside(c):
        return jnp.logical_and(c >= 0, c < NC)

    acc[...] = jnp.zeros_like(acc)

    @pl.loop(0, NC + 2 * E)
    def _(i):
        @pl.when(i < NC)
        def _():
            ffn_copy(0, i).wait()
            gate = jnp.dot(x_all[...], wg[i], preferred_element_type=F32).astype(BF16)
            own[i, 0, :, :CF] = gate[:half]
            own[i, 1, :, :CF] = gate[half:]
            ffn_copy(1, i).wait()
            up = jnp.dot(x_all[...], wu[i], preferred_element_type=F32).astype(BF16)
            own[i, 0, :, CF:] = up[:half]
            own[i, 1, :, CF:] = up[half:]

        for way in (0, 1):
            c = i - (me if way == 0 else E - me)

            @pl.when(inside(c))
            def _():
                sum_stage(way, c)

        for way in (0, 1):
            c = i - E - (me if way == 0 else E - me)

            @pl.when(inside(c))
            def _():
                hid_stage(way, c)

        c = i - E - jnp.maximum(me, E - me)

        @pl.when(inside(c))
        def _():
            ffn_copy(2, c).wait()
            for j in range(NJ):
                cols = slice(j * WC, (j + 1) * WC)
                acc[:, cols] += jnp.dot(hid[c], wd[c, :, cols], preferred_element_type=F32)

    for j in range(NJ):
        cols = slice(j * WC, (j + 1) * WC)
        down[:, cols] = acc[:, cols].astype(BF16)
        for k in range(1, nc):
            rs_copy(k, j, down, down_in, dn_s, dn_r).start()
    for j in range(NJ):
        cols = slice(j * WC, (j + 1) * WC)
        value = stream[:, cols] + acc[my_rows, cols]
        for k in range(1, nc):
            rs_copy(k, j, down, down_in, dn_s, dn_r).wait_recv()
            value = value + down_in[k - 1, :, cols].astype(F32)
        out_ref[:, cols] = value.astype(BF16)

    for k in range(1, nc):
        for j in range(NJ):
            rs_copy(k, j, proj, rs_in, rs_s, rs_r).wait_send()
            x_copy(k, j).wait_send()
            rs_copy(k, j, down, down_in, dn_s, dn_r).wait_send()
        ssc_copy(k).wait_send()

    for a in range(NA):
        @pl.loop(0, nd)
        def _(origin):
            @pl.when(jnp.logical_and(me < E, origin <= me))
            def _():
                att_copy(origin, a, 0, False).wait_send()

            @pl.when(jnp.logical_and(me > 0, origin >= me))
            def _():
                att_copy(origin, a, 1, False).wait_send()

    for way in (0, 1):
        @pl.when(me != (E if way == 0 else 0))
        def _():
            ssd_copy(way).wait_send()

            @pl.loop(0, NC)
            def _(c):
                sum_copy(way, c).wait_send()
                hid_copy(way, c).wait_send()


def layer(nd, nc, attended, seats, resid, gain, w_out, w_gate, w_up, w_down):
    B, HK = attended.shape
    T = seats.shape[1]
    R, DK = resid.shape
    FK = w_gate.shape[1]
    WC = divisor(DK, (512, 256, 128))
    NJ = DK // WC
    AC = divisor(HK, (1024, 512, 256, 128))
    NA = HK // AC
    CF = divisor(FK, (512, 256, 128))
    NC = FK // CF
    half = T // 2
    dims = (T, B, R, HK, WC, NJ, AC, NA, CF, NC, half, float(DK * nd))
    dma = pltpu.SemaphoreType.DMA
    vmem = pl.BlockSpec(memory_space=pltpu.VMEM)
    hbm = pl.BlockSpec(memory_space=pltpu.HBM)
    scratch = [
        pltpu.VMEM((NJ, HK, WC), BF16),
        pltpu.VMEM((NC, DK, CF), BF16),
        pltpu.VMEM((NC, DK, CF), BF16),
        pltpu.VMEM((NC, CF, DK), BF16),
        pltpu.VMEM((T, HK), BF16),
        pltpu.VMEM((T, HK), BF16),
        pltpu.VMEM((T, DK), BF16),
        pltpu.VMEM((nc - 1, R, DK), BF16),
        pltpu.VMEM((T, DK), BF16),
        pltpu.VMEM((T, 128), F32),
        pltpu.VMEM((R, DK), F32),
        pltpu.VMEM((NC, 2, half, 2 * CF), BF16),
        pltpu.VMEM((NC, half, 2 * CF), BF16),
        pltpu.VMEM((NC, half, 2 * CF), BF16),
        pltpu.VMEM((T, 128), F32),
        pltpu.VMEM((half, 128), F32),
        pltpu.VMEM((half, 128), F32),
        pltpu.VMEM((half, 128), F32),
        pltpu.VMEM((NC, T, CF), BF16),
        pltpu.VMEM((T, DK), F32),
        pltpu.VMEM((T, DK), BF16),
        pltpu.VMEM((nc - 1, R, DK), BF16),
        dma((NJ,)),
        dma((3, NC)),
        dma((2, nd, NA)),
        dma((nd, NA)),
        dma((nc - 1, NJ)),
        dma((nc - 1, NJ)),
        dma((nc - 1, NJ)),
        dma((nc - 1, NJ)),
        dma((nc - 1,)),
        dma((nc - 1,)),
        dma((2, NC)),
        dma((2, NC)),
        dma((2,)),
        dma((2,)),
        dma((2, NC)),
        dma((2, NC)),
        dma((nc - 1, NJ)),
        dma((nc - 1, NJ)),
    ]
    return pl.pallas_call(
        functools.partial(layer_kernel, nd, nc, dims),
        out_shape=jax.ShapeDtypeStruct((R, DK), BF16),
        in_specs=[vmem] * 4 + [hbm] * 4,
        out_specs=vmem,
        scratch_shapes=scratch,
        compiler_params=pltpu.CompilerParams(
            collective_id=0, has_side_effects=True, vmem_limit_bytes=67043328
        ),
    )(attended, seats, resid, gain, w_out, w_gate, w_up, w_down)


def solution(mesh):
    nd, nc = mesh.shape["dev"], mesh.shape["col"]

    def on_device(
        queries,
        kv_pages,
        page_table,
        seq_lengths,
        ffn_seat,
        resid,
        w_out,
        norm_gain,
        w_gate,
        w_up,
        w_down,
    ):
        attended = attend(queries, kv_pages, page_table, seq_lengths)
        return layer(
            nd, nc, attended, ffn_seat[None, :], resid, norm_gain[None, :], w_out, w_gate, w_up, w_down
        )

    in_specs = (
        P(("rep", "dev"), "col"),
        P(("rep", "dev"), "col", None, None, None),
        P(("rep", "dev"), None),
        P(("rep", "dev")),
        P("rep"),
        P(("rep", "col"), "dev"),
        P("col", "dev"),
        P("dev"),
        P("dev", "col"),
        P("dev", "col"),
        P("col", "dev"),
    )
    return jax.shard_map(
        on_device,
        mesh=mesh,
        in_specs=in_specs,
        out_specs=P(("rep", "col"), "dev"),
        check_vma=False,
    )
```

time: 219 us -> 126 us (0.58)
  Pallas kernels: 0 us -> 119 us
  waiting for transfers between devices: 82.6 us -> 0 us
  blocking collectives: 54.8 us -> 0 us
  matrix products: 34.4 us -> 0 us
  local copies, waits for them, and re-layouts: 25.2 us -> 6.11 us
  between operations: 13.3 us -> 0.01 us
  other arithmetic: 8.25 us -> 0 us
    pallas_call x0 -> x2, Pallas kernels: none -> 119 us  [the longest x1 92 us: layer(): pl.pallas_call(functools.partial(layer_kernel, nd, nc, dims), out_shape=j...]
    reduce_scatter x3 -> x0, waiting for transfers between devices: 82.5 us -> none  [the longest x1 37.5 us: on_device(): lax.psum_scatter(gate_up.astype(jnp.bfloat16), 'dev', scatter_dimension=0...]
    all_gather x3 -> x0, blocking collectives: 43.2 us -> none  [the longest x1 19.1 us: on_device(): hidden = lax.all_gather(hidden_share, 'dev', axis=0, tiled=True)]
    dot_general x6 -> x0, matrix products: 34.4 us -> none  [the longest x1 8.35 us: on_device(): jnp.dot(hidden, w_down, preferred_element_type=jnp.float32)]
    psum x1 -> x0, blocking collectives: 11.7 us -> none  [on_device(): sq_total = lax.psum(jnp.sum(stream * stream, axis=1), 'dev')]
    gather x1 -> x0, local copies, waits for them, and re-layouts: 11.5 us -> none  [on_device(): kv_blocks = kv_pages[page_table]]
    slice x1 -> x0, local copies, waits for them, and re-layouts: 5.33 us -> none  [on_device(): kv_blocks[:, :, :, 0].transpose(0, 2, 1, 3, 4)]
    convert_element_type x5 -> x0, other arithmetic: 4.67 us -> none  [the longest x1 1.61 us: on_device(): return (stream + ffn_out).astype(jnp.bfloat16)]
  transfers between devices with their start and end apart: 3 -> 0, of which waited for: 3 -> 0; matrix products, arithmetic and copies ran while one was open for 0% -> 0% of each run, Pallas kernels for 0% -> 0%
where the time goes in v1:
time: 126 us
  Pallas kernels  119 us (94%)
  local copies, waits for them, and re-layouts  6.11 us (5%)
    pallas_call x1, Pallas kernels, layer(): pl.pallas_call(functools.partial(layer_kernel, nd, nc, dims), out_shape=j...  92 us
    pallas_call x1, Pallas kernels, attend(): pl.pallas_call(functools.partial(attend_kernel, seqs, pages, kv_local), g...  27.5 us
    unnamed x4, local copies, waits for them, and re-layouts  5.5 us

profile of v1, /device:TPU:0, one launch (start us, length us, event | category | flops | bytes accessed | tf_op | source)
XLA Modules:
  0.0 125.6 jit_solution(12066291965977303505)
XLA Ops:
  0.0 0.8 copy.13
  0.8 0.6 reshape.9.table_ref
  1.4 1.6 %copy.14 = bf16[4,8,16,128]{3,2,1,0:T(8,128)(2,1)} copy(bf16[4,8,16,128]{3,1,2,0:T(8,128)(2,1)} %bitcast.13) | data formatting | bytes 262144
  3.0 27.5 %shard_map.109 = bf16[32,2,8,128]{3,2,1,0:T(8,128)(2,1)} custom-call(s32[96]{0:T(128)} %reshape.9.table_ref, s32[32]{0:T(128)} %len_ref.1, bf16[32,2,8,128]{3,2,1,0:T(8,128)(2,1)} %bitcast.12, bf16[96,2,2,128,128]{4,3,2,1,0:T(8,128)(2,1)} %refs_11_.1, bf16[96,2,2,128,128]{4,3,2,1,0:T(8,128)(2,1)} %refs_11_.1, bf16[96,2,2,128,128]{4,3,2,1,0:T(8,128)(2,1)} %refs_11_.1, ...), custom_call_target="tpu_custom_call" | custom-call | tf_op jit(solution)/shard_map/pallas_call | solution.py:76
  30.5 1.6 %copy.17 = bf16[4,8,16,128]{3,1,2,0:T(8,128)(2,1)} copy(bf16[4,8,16,128]{3,2,1,0:T(8,128)(2,1)} %bitcast.11) | data formatting | bytes 262144
  32.1 92.0 %shard_map.110 = bf16[32,2048]{1,0:T(8,128)(2,1)} custom-call(bf16[32,2048]{1,0:T(8,128)(2,1)} %bitcast.10, s32[1,128]{1,0:T(1,128)} %bitcast.15, bf16[32,2048]{1,0:T(8,128)(2,1)} %resid_ref.1, f32[1,2048]{1,0:T(1,128)} %bitcast.14, bf16[2048,2048]{1,0:T(8,128)(2,1)} %wo_hbm.1, bf16[2048,3584]{1,0:T(8,128)(2,1)} %wg_hbm.1, bf16[2048,3584]{1,0:T(8,128)(2,1)} %wu_hbm.1, ...), custom_call_target="tpu_custom_call" | custom-call | tf_op jit(solution)/shard_map/pallas_call | solution.py:542
  124.1 1.6 %copy.19 = bf16[32,2048]{1,0:T(8,128)(2,1)} copy(bf16[32,2048]{1,0:T(8,128)(2,1)} %shard_map.110) | data formatting | bytes 262144
